TPU v7x, 128 devices: a whole 4x4x4 slice. The times are simulated.
128 devices in a mesh: dp: 16 (over y_hi, z, core), tensor: 8 (over y_lo, x).
Axes of the slice: x: 4, y: 4 (y_hi: 2, y_lo: 2; y = y_hi * 2 + y_lo), z: 4, core: 2. Of those that a mesh axis runs over, the one named last changes fastest.
Arguments:
- saved_queries: bfloat16 [16384, 8192], P('dp', 'tensor'), may hold values from -200 to 200
- saved_keys: bfloat16 [16384, 1024], P('dp', 'tensor'), may hold values from -200 to 200
- saved_values: bfloat16 [16384, 1024], P('dp', 'tensor'), may hold values from -6 to 6
- out_grad: bfloat16 [16384, 8192], P(('dp', 'tensor')), may hold values from -2.5 to 2.5
- act_exponent: int32 [1], replicated, may hold values from -6 to 3
- grad_exponent: int32 [1], replicated, may hold values from -4 to 1
Outputs:
- grad_weight: float32 [8192, 8192], P('dp', 'tensor')
All inputs are finite; a program needn't handle non-finite values.
Results may differ from a plain program's by a relative error of at most 0.012.
Values may be sent and summed in bfloat16 or wider, within the bound.
A program may use at most 128 MiB of HBM per device.

v0:
```python
import jax
import jax.numpy as jnp
from jax import lax
from jax.sharding import PartitionSpec as P

HEAD_DIM = 128
SATURATION = 448.0


def quantize(values_in, exponent):
    factor = SATURATION * jnp.exp2(-exponent[0].astype(jnp.float32))
    return jnp.clip(values_in * factor, -SATURATION, SATURATION).astype(jnp.bfloat16)


def attend(query_rows, key_rows, value_rows):
    scores = jnp.dot(query_rows, key_rows.T, preferred_element_type=jnp.float32) * HEAD_DIM ** (
        -0.5
    )
    positions = jnp.arange(query_rows.shape[0], dtype=jnp.int32)
    causal = positions[None, :] <= positions[:, None]
    scores = jnp.where(causal, scores, jnp.float32(-1e30))
    row_max = jnp.max(scores, axis=1, keepdims=True)
    weights = jnp.exp(scores - row_max)
    probabilities = (weights / jnp.sum(weights, axis=1, keepdims=True)).astype(jnp.bfloat16)
    return jnp.dot(probabilities, value_rows, preferred_element_type=jnp.float32)


def on_device(saved_queries, saved_keys, saved_values, out_grad, act_exponent, grad_exponent):
    seq_len = saved_queries.shape[0]
    local_width = saved_queries.shape[1]
    heads_here = local_width // HEAD_DIM
    dequant = jnp.exp2((act_exponent[0] + grad_exponent[0]).astype(jnp.float32)) / (
        SATURATION * SATURATION
    )

    def one_head(head_index, scaled_rows):
        query_rows = lax.dynamic_slice_in_dim(saved_queries, head_index * HEAD_DIM, HEAD_DIM, 1)
        attended = attend(query_rows, saved_keys, saved_values)
        return lax.dynamic_update_slice_in_dim(
            scaled_rows, quantize(attended, act_exponent), head_index * HEAD_DIM, 1
        )

    act_scaled = lax.fori_loop(
        0, heads_here, one_head, jnp.zeros((seq_len, local_width), jnp.bfloat16)
    )
    grad_scaled = quantize(out_grad.astype(jnp.float32), grad_exponent)
    running = lax.dot_general(
        lax.all_gather(grad_scaled, "tensor", axis=0, tiled=True),
        act_scaled,
        (((0,), (0,)), ((), ())),
        preferred_element_type=jnp.float32,
    )
    grad_weight = lax.psum_scatter(
        (running * dequant).astype(jnp.bfloat16), "dp", scatter_dimension=0, tiled=True
    ).astype(jnp.float32)
    return grad_weight


def solution(mesh):
    in_specs = (
        P("dp", "tensor"),
        P("dp", "tensor"),
        P("dp", "tensor"),
        P(("dp", "tensor"), None),
        P(),
        P(),
    )
    out_specs = P("dp", "tensor")
    return jax.shard_map(
        on_device, mesh=mesh, in_specs=in_specs, out_specs=out_specs, check_vma=False
    )
```

profile of v0, /device:TPU:0, one launch (start us, length us, event | category | flops | bytes accessed | tf_op | source)
XLA Modules:
  0.0 367.2 jit_solution(14772406896722090747)
XLA Ops:
  7.3 3.5 clamp_convert_fusion
  11.8 25.3 %while.15 = (s32[]{:T(128)}, bf16[1024,1024]{1,0:T(8,128)(2,1)S(1)}, bf16[1024,1024]{1,0:T(8,128)(2,1)}, bf16[1024,128]{1,0:T(8,128)(2,1)S(1)}, bf16[1024,128]{1...) while((s32[]{:T(128)}, bf16[1024,1024]{1,0:T(8,128)(2,1)S(1)}, ...), condition=%wide.region_3.4_spmd, body=%wide.region_0.3_spmd.sunk | while | flops 552990720 | bytes 13652127 | solution.py:43
  11.9 1.7 fusion.23
  14.1 0.9 fusion.25
  15.0 1.7 fusion.23
  17.2 0.9 fusion.25
  18.2 1.7 fusion.23
  20.4 0.9 fusion.25
  21.3 1.7 fusion.23
  23.0 0.5 fusion.24
  23.6 0.9 fusion.25
  24.5 1.7 fusion.23
  26.2 0.5 fusion.24
  26.7 0.9 fusion.25
  27.7 1.7 fusion.23
  29.9 0.9 fusion.25
  30.8 1.7 fusion.23
  33.0 0.9 fusion.25
  34.0 1.7 fusion.23
  36.2 0.9 fusion.25
  37.1 146.7 %all-gather.2.cloned.1.call-done = bf16[1024,8192]{1,0:T(8,128)(2,1)} async-done(((bf16[128,8192]{1,0:T(8,128)(2,1)}), bf16[1024,8192]{1,0:T(8,128)(2,1)}) %all-gather.2.cloned.1.call-update) | async-done | bytes 16777232 | tf_op jit(solution)/shard_map/all_gather | solution.py:48
  183.9 27.4 %multiply_convert_fusion = bf16[8192,1024]{1,0:T(8,128)(2,1)} fusion(bf16[1024,8192]{1,0:T(8,128)(2,1)} %all-gather.2.cloned.1.call-done, bf16[1024,1024]{1,0:T(8,128)(2,1)S(1)} %get-tuple-element.158, f32[]{:T(128)} %bitcast.2), kind=kOutput, calls=%fused_computation.16 | convolution fusion | flops 17196646400 | bytes 35651588 | tf_op jit(solution)/shard_map/dot_general | solution.py:47
  211.3 146.3 %reduce-scatter.2.cloned.1.call-done = bf16[512,1024]{1,0:T(8,128)(2,1)} async-done(((bf16[8192,1024]{1,0:T(8,128)(2,1)}), bf16[512,1024]{1,0:T(8,128)(2,1)}) %reduce-scatter.2.cloned.1.call-update) | async-done | bytes 1048592 | tf_op jit(solution)/shard_map/reduce_scatter | solution.py:53
  357.6 2.8 convert_element_type.54
  (15 shorter events, 3.5 us)
Async XLA Ops:
  6.5 177.3 %all-gather.2.cloned.1.call-start = ((), (), s32[]{:S(2)}) async-start(), calls=%async_computation.1 | async-start | bytes 18874368 | tf_op jit(solution)/shard_map/all_gather | solution.py:48
  7.2 4.6 %copy-start = (bf16[1024,128]{1,0:T(8,128)(2,1)S(1)}, bf16[1024,128]{1,0:T(8,128)(2,1)}, u32[]{:S(2)}) copy-start(bf16[1024,128]{1,0:T(8,128)(2,1)} %param.9) | copy-start | bytes 786436
  7.2 4.6 %copy-start.1 = (bf16[1024,128]{1,0:T(8,128)(2,1)S(1)}, bf16[1024,128]{1,0:T(8,128)(2,1)}, u32[]{:S(2)}) copy-start(bf16[1024,128]{1,0:T(8,128)(2,1)} %param.10) | copy-start | bytes 786436
  10.8 346.8 %reduce-scatter.2.cloned.1.call-start = ((), (), s32[]{:S(2)}) async-start(), calls=%async_computation.2 | async-start | bytes 17825792 | tf_op jit(solution)/shard_map/reduce_scatter | solution.py:53
Sparse Core Ops, SparseCore 0:
  10.9 172.9 all-gather.1
  211.4 146.1 reduce-scatter.1
where the time goes:
time: 368 us; the launch traced here: 367 us
  waiting for transfers between devices  293 us (80%)
  matrix products  48.3 us (13%)
  between operations  14.9 us (4%)
  other arithmetic  10.5 us (3%)
    all_gather x1, waiting for transfers between devices, on_device(): lax.all_gather(grad_scaled, 'tensor', axis=0, tiled=True)  147 us
    reduce_scatter x1, waiting for transfers between devices, on_device(): lax.psum_scatter((running * dequant).astype(jnp.bfloat16), 'dp', scatter_...  146 us
    dot_general x1, matrix products, on_device(): lax.dot_general(lax.all_gather(grad_scaled, 'tensor', axis=0, tiled=True)...  27.4 us
    dot_general x8, matrix products, attend(): jnp.dot(query_rows, key_rows.T, preferred_element_type=jnp.float32)  13.4 us
    dot_general x8, matrix products, attend(): jnp.dot(probabilities, value_rows, preferred_element_type=jnp.float32)  7.5 us
  transfers between devices with their start and end apart: 2, of which 2 were waited for; matrix products, arithmetic and copies ran while one was open for 7% of the time, Pallas kernels for 0%

commit v1 on v0

--- a/solution.py
+++ b/solution.py
@@ -45,7 +45,15 @@
     )
     grad_scaled = quantize(out_grad.astype(jnp.float32), grad_exponent)
     running = lax.dot_general(
-        lax.all_gather(grad_scaled, "tensor", axis=0, tiled=True),
+        jnp.concatenate(
+            lax.all_to_all(
+                jnp.stack(lax.axis_size("tensor") * [grad_scaled], 0),
+                "tensor",
+                split_axis=0,
+                concat_axis=0,
+            ),
+            axis=0,
+        ),
         act_scaled,
         (((0,), (0,)), ((), ())),
         preferred_element_type=jnp.float32,

time: 368 us -> 459 us (1.25)
  waiting for transfers between devices: 293 us -> 374 us
  local copies, waits for them, and re-layouts: 0.26 us -> 6.22 us
  starting transfers between devices: 0.04 us -> 5.92 us
    all_to_all x0 -> x1, waiting for transfers between devices: none -> 158 us  [on_device(): lax.all_to_all(jnp.stack(lax.axis_size('tensor') * [grad_scaled], 0), 'te...]
    all_gather x1 -> x0, waiting for transfers between devices: 147 us -> none  [on_device(): lax.all_gather(grad_scaled, 'tensor', axis=0, tiled=True)]
    reduce_scatter x1, waiting for transfers between devices: 146 us -> 216 us  [on_device(): lax.psum_scatter((running * dequant).astype(jnp.bfloat16), 'dp', scatter_...]
    another operation x0 -> x1, local copies, waits for them, and re-layouts: none -> 5.96 us  [on_device(): jnp.stack(lax.axis_size('tensor') * [grad_scaled], 0)]
    all_to_all x0 -> x1, starting transfers between devices: none -> 5.88 us  [on_device(): lax.all_to_all(jnp.stack(lax.axis_size('tensor') * [grad_scaled], 0), 'te...]
  transfers between devices with their start and end apart: 2 -> 2, of which waited for: 2 -> 2; matrix products, arithmetic and copies ran while one was open for 7% -> 6% of each run, Pallas kernels for 0% -> 0%
where the time goes in v1:
time: 459 us
  waiting for transfers between devices  374 us (81%)
  matrix products  48.2 us (11%)
  between operations  14.9 us (3%)
  other arithmetic  9.09 us (2%)
  local copies, waits for them, and re-layouts  6.22 us (1%)
  starting transfers between devices  5.92 us (1%)
    reduce_scatter x1, waiting for transfers between devices, on_device(): lax.psum_scatter((running * dequant).astype(jnp.bfloat16), 'dp', scatter_...  216 us
    all_to_all x1, waiting for transfers between devices, on_device(): lax.all_to_all(jnp.stack(lax.axis_size('tensor') * [grad_scaled], 0), 'te...  158 us
    dot_general x1, matrix products, on_device(): lax.dot_general(jnp.concatenate(lax.all_to_all(jnp.stack(lax.axis_size('t...  27.4 us
    dot_general x8, matrix products, attend(): jnp.dot(query_rows, key_rows.T, preferred_element_type=jnp.float32)  13.4 us
  transfers between devices with their start and end apart: 2, of which 2 were waited for; matrix products, arithmetic and copies ran while one was open for 6% of the time, Pallas kernels for 0%

profile of v1, /device:TPU:0, one launch (start us, length us, event | category | flops | bytes accessed | tf_op | source)
XLA Modules:
  0.0 458.8 jit_solution(8610701257877056660)
XLA Ops:
  7.2 2.1 clamp_convert_fusion
  9.3 6.0 %stack.2 = bf16[8,128,8192]{2,1,0:T(8,128)(2,1)} broadcast(bf16[128,8192]{1,0:T(8,128)(2,1)S(1)} %clamp_convert_fusion), dimensions={1,2} | broadcast | bytes 18874368 | tf_op jit(solution)/shard_map/stack | solution.py:50
  15.3 5.9 %all-to-all-start = ((bf16[8,128,8192]{2,1,0:T(8,128)(2,1)}), bf16[8,128,8192]{2,1,0:T(8,128)(2,1)}, u32[]{:S(2)}, u32[]{:S(2)}) async-start(bf16[8,128,8192]{2,1,0:T(8,128)(2,1)} %stack.2), calls=%async_computation | async-start | bytes 33554432 | tf_op jit(solution)/shard_map/all_to_all | solution.py:49
  22.3 25.3 %while.15 = (s32[]{:T(128)}, bf16[1024,1024]{1,0:T(8,128)(2,1)S(1)}, bf16[1024,1024]{1,0:T(8,128)(2,1)}, bf16[1024,128]{1,0:T(8,128)(2,1)S(1)}, bf16[1024,128]{1...) while((s32[]{:T(128)}, bf16[1024,1024]{1,0:T(8,128)(2,1)S(1)}, ...), condition=%wide.region_3.4_spmd, body=%wide.region_0.3_spmd.sunk | while | flops 552990720 | bytes 13652127 | solution.py:43
  22.3 1.7 fusion.23
  24.5 0.9 fusion.25
  25.4 1.7 fusion.23
  27.6 0.9 fusion.25
  28.6 1.7 fusion.23
  30.8 0.9 fusion.25
  31.8 1.7 fusion.23
  34.0 0.9 fusion.25
  34.9 1.7 fusion.23
  37.1 0.9 fusion.25
  38.1 1.7 fusion.23
  40.3 0.9 fusion.25
  41.2 1.7 fusion.23
  43.4 0.9 fusion.25
  44.4 1.7 fusion.23
  46.6 0.9 fusion.25
  47.5 158.2 %all-to-all-done = bf16[8,128,8192]{2,1,0:T(8,128)(2,1)} async-done(((bf16[8,128,8192]{2,1,0:T(8,128)(2,1)}), bf16[8,128,8192]{2,1,0:T(8,128)(2,1)}, u32[]{:S(2)}, u32[]{:S(2)}) %all-to-all-start) | async-done | bytes 16777248 | tf_op jit(solution)/shard_map/all_to_all | solution.py:49
  205.8 27.4 %multiply_convert_fusion = bf16[8192,1024]{1,0:T(8,128)(2,1)} fusion(bf16[1024,8192]{1,0:T(8,128)(2,1)} %bitcast.1, bf16[1024,1024]{1,0:T(8,128)(2,1)S(1)} %get-tuple-element.158, f32[]{:T(128)} %bitcast.3), kind=kOutput, calls=%fused_computation.16 | convolution fusion | flops 17196646400 | bytes 35651588 | tf_op jit(solution)/shard_map/dot_general | solution.py:47
  233.2 216.0 %reduce-scatter.2.cloned.1.call-done = bf16[512,1024]{1,0:T(8,128)(2,1)} async-done(((bf16[8192,1024]{1,0:T(8,128)(2,1)}), bf16[512,1024]{1,0:T(8,128)(2,1)}) %reduce-scatter.2.cloned.1.call-update) | async-done | bytes 1048592 | tf_op jit(solution)/shard_map/reduce_scatter | solution.py:61
  449.2 2.8 convert_element_type.54
  (15 shorter events, 4.5 us)
Async XLA Ops:
  15.3 6.9 %copy-start = (bf16[1024,128]{1,0:T(8,128)(2,1)S(1)}, bf16[1024,128]{1,0:T(8,128)(2,1)}, u32[]{:S(2)}) copy-start(bf16[1024,128]{1,0:T(8,128)(2,1)} %param.9) | copy-start | bytes 786436
  15.3 7.0 %copy-start.1 = (bf16[1024,128]{1,0:T(8,128)(2,1)S(1)}, bf16[1024,128]{1,0:T(8,128)(2,1)}, u32[]{:S(2)}) copy-start(bf16[1024,128]{1,0:T(8,128)(2,1)} %param.10) | copy-start | bytes 786436
  15.3 190.4 %all-to-all-start = ((bf16[8,128,8192]{2,1,0:T(8,128)(2,1)}), bf16[8,128,8192]{2,1,0:T(8,128)(2,1)}, u32[]{:S(2)}, u32[]{:S(2)}) async-start(bf16[8,128,8192]{2,1,0:T(8,128)(2,1)} %stack.2), calls=%async_computation | async-start | bytes 33554432 | tf_op jit(solution)/shard_map/all_to_all | solution.py:49
  21.2 427.9 %reduce-scatter.2.cloned.1.call-start = ((), (), s32[]{:S(2)}) async-start(), calls=%async_computation.2 | async-start | bytes 17825792 | tf_op jit(solution)/shard_map/reduce_scatter | solution.py:61
Sparse Core Ops, SparseCore 0:
  233.3 215.8 reduce-scatter.1
